TPU v7x, 32 devices: a whole 2x2x4 slice. The times are simulated.
32 devices in a mesh: seqa: 4 (over z), seqb: 2 (over x), dp: 4 (over y, core).
Axes of the slice: x: 2, y: 2, z: 4, core: 2. Of those that a mesh axis runs over, the one named last changes fastest.
Arguments:
- queries: bfloat16 [1024, 8, 64], P(('dp', 'seqa', 'seqb')), parts along dimension 0, may hold values from -6 to 6
- keys: bfloat16 [1024, 8, 64], P(('dp', 'seqa', 'seqb')), parts along dimension 0, may hold values from -6 to 6
- values: bfloat16 [1024, 8, 64], P(('dp', 'seqa', 'seqb')), parts along dimension 0, may hold values from -6 to 6
- doc_bounds: int32 [36], P('dp'), parts along dimension 0, may hold values from 0 to 256, as said below
- q_gain: float32 [64], replicated, may hold values from 0.25 to 1.75
- k_gain: float32 [64], replicated, may hold values from 0.25 to 1.75
Outputs:
- attended: bfloat16 [1024, 8, 64], P(('dp', 'seqa', 'seqb')), parts along dimension 0
There are 4 independent parts, one for each index of `dp`. A program takes and returns all parts, laid end to end along the dimension named above; an argument that names none is the same for every part. Nothing has to cross between parts.
Inputs may be any that keep to these rules, and one draw needn't show every extreme that they name: doc_bounds[0] is 0, doc_bounds[8] is 256, and the entries rise strictly.
All inputs are finite; a program needn't handle non-finite values.
Results may differ from a plain program's by a relative error of at most 0.0015.
Values may be sent and summed in bfloat16 or wider, within the bound.
A program may use at most 64 MiB of HBM per device.

v0:
```python
import jax
import jax.numpy as jnp
from jax import lax
from jax.sharding import PartitionSpec as P

TOK_DEV = 32
DOCS = 8


def for_sending(value):
    return jax.tree.map(lambda a: a.astype(jnp.bfloat16) if a.dtype == jnp.float32 else a, value)


def prepare(block, gain, positions):
    values32 = block.astype(jnp.float32)
    scale = lax.rsqrt(jnp.mean(values32 * values32, axis=-1, keepdims=True) + 1e-06)
    normed = values32 * scale * gain
    half = normed.shape[-1] // 2
    freq = jnp.exp(-jnp.log(10000.0) * jnp.arange(half, dtype=jnp.float32) * 2.0 / normed.shape[-1])
    angle = positions.astype(jnp.float32)[:, None] * freq[None, :]
    first = normed[:, :half]
    second = normed[:, half:]
    cosine = jnp.cos(angle)
    sine = jnp.sin(angle)
    rotated = jnp.concatenate(
        [first * cosine - second * sine, first * sine + second * cosine], axis=-1
    )
    return rotated.astype(jnp.bfloat16)


def attend_head(query_head, key_head, value_head, doc_bounds, q_gain, k_gain):
    length, width = query_head.shape
    places = jnp.arange(length, dtype=jnp.int32)
    doc = jnp.sum((places[:, None] >= doc_bounds[None, 1:DOCS]).astype(jnp.int32), axis=1).astype(
        jnp.int32
    )
    positions = places - doc_bounds[doc]
    qr = prepare(query_head, q_gain, positions)
    kr = prepare(key_head, k_gain, positions)
    block = 8 * TOK_DEV
    count = length // block

    def one_block(items):
        query_rows, query_doc, query_place = items
        scores = jnp.dot(query_rows, kr.T, preferred_element_type=jnp.float32) / jnp.sqrt(
            jnp.float32(width)
        )
        allowed = (query_doc[:, None] == doc[None, :]) & (places[None, :] <= query_place[:, None])
        scores = jnp.where(allowed, scores, jnp.float32(-1e30))
        top = jnp.max(scores, axis=1, keepdims=True)
        expo = jnp.where(allowed, jnp.exp(scores - top), jnp.float32(0.0))
        weights = (expo / jnp.sum(expo, axis=1, keepdims=True)).astype(jnp.bfloat16)
        return jnp.dot(weights, value_head, preferred_element_type=jnp.float32).astype(jnp.bfloat16)

    outputs = lax.map(
        one_block,
        (qr.reshape(count, block, width), doc.reshape(count, block), places.reshape(count, block)),
    )
    return outputs.reshape(length, width)


def body(queries, keys, values, doc_bounds, q_gain, k_gain):
    query_full, key_full, value_full = (
        lax.all_to_all(queries, ("seqa", "seqb"), split_axis=1, concat_axis=0, tiled=True),
        lax.all_to_all(keys, ("seqa", "seqb"), split_axis=1, concat_axis=0, tiled=True),
        lax.all_to_all(values, ("seqa", "seqb"), split_axis=1, concat_axis=0, tiled=True),
    )
    attend_all = jax.vmap(attend_head, in_axes=(1, 1, 1, None, None, None), out_axes=1)
    result = attend_all(query_full, key_full, value_full, doc_bounds, q_gain, k_gain)
    back = jax.tree.map(
        lambda part, own: part.astype(own.dtype),
        lax.all_to_all(
            for_sending(result), ("seqa", "seqb"), split_axis=0, concat_axis=1, tiled=True
        ),
        result,
    )
    return back


def solution(mesh):
    placed = (
        P(("dp", "seqa", "seqb"), None, None),
        P(("dp", "seqa", "seqb"), None, None),
        P(("dp", "seqa", "seqb"), None, None),
        P("dp"),
        P(),
        P(),
    )
    return jax.shard_map(
        body,
        mesh=mesh,
        in_specs=placed,
        out_specs=P(("dp", "seqa", "seqb"), None, None),
        check_vma=False,
    )
```

profile of v0, /device:TPU:0, one launch (start us, length us, event | category | flops | bytes accessed | tf_op | source)
XLA Modules:
  0.0 51.4 jit_solution(5390356876942272930)
XLA Ops:
  0.0 0.8 %copy.39 = bf16[32,8,64]{2,0,1:T(8,128)(2,1)S(1)} copy(bf16[32,8,64]{2,1,0:T(8,128)(2,1)} %param.6) | data formatting | bytes 65536 | tf_op args[0]
  0.9 0.7 %reshape.437 = bf16[8,2,1024]{2,1,0:T(2,128)(2,1)} reshape(bf16[8,32,64]{2,1,0:T(8,128)(2,1)S(1)} %bitcast.69) | data formatting | bytes 65536
  1.6 7.4 %all-to-all-start = ((bf16[8,2,1024]{2,1,0:T(2,128)(2,1)}), bf16[8,2,1024]{2,1,0:T(2,128)(2,1)S(1)}, u32[]{:S(2)}, u32[]{:S(2)}) async-start(bf16[8,2,1024]{2,1,0:T(2,128)(2,1)} %reshape.437), calls=%async_computation | async-start | bytes 65536 | tf_op jit(solution)/shard_map/all_to_all | solution.py:64
  9.0 0.7 %fusion.35 = (s32[1]{0:T(128)}, s32[1]{0:T(128)}, s32[1]{0:T(128)}, s32[1]{0:T(128)}, s32[1]{0:T(128)}, /*index=5*/s32[1]{0:T(128)}, s32[1]{0:T(128)}, s32[1]{0:T(128)}, s32[1]{0:T(128)}) fusion(s32[9]{0:T(128)S(1)} %copy-done.2), kind=kLoop, calls=%fused_computation.61 | loop fusion | bytes 72 | tf_op jit(solution)/shard_map/vmap()/gather | solution.py:37
  9.9 0.7 %reshape.439 = bf16[8,2,1024]{2,1,0:T(2,128)(2,1)} reshape(bf16[8,32,64]{2,1,0:T(8,128)(2,1)S(1)} %bitcast.70) | data formatting | bytes 65536
  10.6 0.1 copy-done.1
  10.7 0.7 %reshape.435 = bf16[8,2,1024]{2,1,0:T(2,128)(2,1)} reshape(bf16[8,32,64]{2,1,0:T(8,128)(2,1)S(1)} %bitcast.71) | data formatting | bytes 65536
  11.5 4.4 %compare_select_fusion.1 = s32[256,1]{0,1:T(1,128)S(1)} fusion(s32[]{:T(128)} %bitcast.7, s32[]{:T(128)} %bitcast.8, s32[]{:T(128)} %bitcast.9, s32[]{:T(128)} %bitcast.10, s32[]{:T(128)} %bitcast.11, s32[]{:T(128)} %bitcast.13, s32[]{:T(128)} %bitcast.12, s32[256,1]{0,1:T(1,128)S(1)} %bitcast.74), kind=kLoop, calls=%fused_computation.50 | loop fusion | flops 3840 | bytes 2076 | tf_op jit(solution)/shard_map/vmap()/gather | solution.py:37
  15.8 1.2 %fusion.32 = f32[256]{0:T(256)S(1)} fusion(pred[256]{0:T(512)(128)(4,1)S(1)} %get-tuple-element.22, pred[256]{0:T(512)(128)(4,1)S(1)} %get-tuple-element.21, s32[256]{0:T(256)S(1)} %bitcast.75, s32[]{:T(128)} %bitcast.5, s32[]{:T(128)} %bitcast.6), kind=kLoop, calls=%fused_computation.57 | loop fusion | flops 1024 | bytes 2568 | tf_op jit(solution)/shard_map/vmap()/convert_element_type | solution.py:20
  17.1 6.0 %all-to-all-start.1 = ((bf16[8,2,1024]{2,1,0:T(2,128)(2,1)}), bf16[8,2,1024]{2,1,0:T(2,128)(2,1)S(1)}, u32[]{:S(2)}, u32[]{:S(2)}) async-start(bf16[8,2,1024]{2,1,0:T(2,128)(2,1)} %reshape.439), calls=%async_computation.1 | async-start | bytes 65536 | tf_op jit(solution)/shard_map/all_to_all | solution.py:65
  23.6 6.2 %all-to-all-done.1 = bf16[8,2,1024]{2,1,0:T(2,128)(2,1)S(1)} async-done(((bf16[8,2,1024]{2,1,0:T(2,128)(2,1)}), bf16[8,2,1024]{2,1,0:T(2,128)(2,1)S(1)}, u32[]{:S(2)}, u32[]{:S(2)}) %all-to-all-start.1) | async-done | bytes 32800 | tf_op jit(solution)/shard_map/all_to_all | solution.py:65
  29.8 3.3 %all-to-all-start.2 = ((bf16[8,2,1024]{2,1,0:T(2,128)(2,1)}), bf16[8,2,1024]{2,1,0:T(2,128)(2,1)S(1)}, u32[]{:S(2)}, u32[]{:S(2)}) async-start(bf16[8,2,1024]{2,1,0:T(2,128)(2,1)} %reshape.435), calls=%async_computation.2 | async-start | bytes 65536 | tf_op jit(solution)/shard_map/all_to_all | solution.py:66
  33.6 0.6 %copy-done.3 = f32[64]{0:T(128)S(1)} copy-done((f32[64]{0:T(128)S(1)}, f32[64]{0:T(128)}, u32[]{:S(2)}) %copy-start.3) | copy-done | bytes 280
  34.2 0.1 fusion.20
  34.4 0.6 %fusion.29 = (bf16[256,32]{1,0:T(8,128)(2,1)S(1)}, bf16[256,32]{1,0:T(8,128)(2,1)S(1)}, bf16[256,32]{1,0:T(8,128)(2,1)S(1)}, bf16[256,32]{1,0:T(8,128)(2,1)S(1)}) fusion(f32[1,256,64]{2,1,0:T(8,128)S(1)} %get-tuple-element.51, f32[32]{0:T(128)S(1)} %multiply_exponential_fusion, f32[256]{0:T(256)S(1)} %fusion.32, f32[1,256,64]{2,1,0:T(8,128)S(1)} %get-tuple-element.52), kind=kLoop, calls=%fused_computation.40 | loop fusion | flops 139264 | bytes 197760 | tf_op jit(solution)/shard_map/vmap()/concatenate | solution.py:25
  35.0 0.3 fusion.36
  35.3 0.1 fusion.11
  35.4 4.4 %all-to-all-done.2 = bf16[8,2,1024]{2,1,0:T(2,128)(2,1)S(1)} async-done(((bf16[8,2,1024]{2,1,0:T(2,128)(2,1)}), bf16[8,2,1024]{2,1,0:T(2,128)(2,1)S(1)}, u32[]{:S(2)}, u32[]{:S(2)}) %all-to-all-start.2) | async-done | bytes 32800 | tf_op jit(solution)/shard_map/all_to_all | solution.py:66
  39.9 0.2 fusion.1
  40.1 0.5 broadcast.313
  40.7 0.7 %reduce.16 = bf16[256,64]{0,1:T(8,128)(2,1)S(1)} reduce(bf16[256,1,64]{0,2,1:T(8,128)(2,1)S(1)} %fusion.1, bf16[]{:T(256)} %broadcast.313), dimensions={1}, to_apply=%copy.29.reduce_sub_computation | reduce | bytes 65538 | tf_op jit(solution)/shard_map/vmap()/transpose;vmap()/reshape;vmap()/transpose | solution.py:69
  41.4 0.1 reshape.441
  41.6 9.1 %all_to_all.51 = bf16[8,2,1024]{2,1,0:T(2,128)(2,1)S(1)} all-to-all(bf16[8,2,1024]{2,1,0:T(2,128)(2,1)S(1)} %reshape.441), channel_id=1, replica_groups=mesh['seqa'=4,'seqb'=2,'dp'=4] {'seqa','seqb'}, dimensions={0} | all-to-all | bytes 65536 | tf_op jit(solution)/shard_map/all_to_all | solution.py:72
  50.8 0.7 %copy.30 = bf16[32,8,64]{2,1,0:T(8,128)(2,1)} copy(bf16[32,8,64]{2,0,1:T(8,128)(2,1)S(1)} %bitcast.68) | data formatting | bytes 65536 | tf_op jit(solution)/shard_map/all_to_all | solution.py:72
  (31 shorter events, 1.5 us)
Async XLA Ops:
  0.9 8.1 %copy-start.2 = (s32[9]{0:T(128)S(1)}, s32[9]{0:T(128)}, u32[]{:S(2)}) copy-start(s32[9]{0:T(128)} %param.9) | copy-start | bytes 112
  1.6 8.3 %copy-start = (bf16[32,8,64]{2,1,0:T(8,128)(2,1)S(1)}, bf16[32,8,64]{2,1,0:T(8,128)(2,1)}, u32[]{:S(2)}) copy-start(bf16[32,8,64]{2,1,0:T(8,128)(2,1)} %param.7) | copy-start | bytes 98308
  1.6 15.5 %all-to-all-start = ((bf16[8,2,1024]{2,1,0:T(2,128)(2,1)}), bf16[8,2,1024]{2,1,0:T(2,128)(2,1)S(1)}, u32[]{:S(2)}, u32[]{:S(2)}) async-start(bf16[8,2,1024]{2,1,0:T(2,128)(2,1)} %reshape.437), calls=%async_computation | async-start | bytes 65536 | tf_op jit(solution)/shard_map/all_to_all | solution.py:64
  9.9 0.8 %copy-start.1 = (bf16[32,8,64]{2,1,0:T(8,128)(2,1)S(1)}, bf16[32,8,64]{2,1,0:T(8,128)(2,1)}, u32[]{:S(2)}) copy-start(bf16[32,8,64]{2,1,0:T(8,128)(2,1)} %param.8) | copy-start | bytes 98308
  17.1 12.7 %all-to-all-start.1 = ((bf16[8,2,1024]{2,1,0:T(2,128)(2,1)}), bf16[8,2,1024]{2,1,0:T(2,128)(2,1)S(1)}, u32[]{:S(2)}, u32[]{:S(2)}) async-start(bf16[8,2,1024]{2,1,0:T(2,128)(2,1)} %reshape.439), calls=%async_computation.1 | async-start | bytes 65536 | tf_op jit(solution)/shard_map/all_to_all | solution.py:65
  29.8 10.0 %all-to-all-start.2 = ((bf16[8,2,1024]{2,1,0:T(2,128)(2,1)}), bf16[8,2,1024]{2,1,0:T(2,128)(2,1)S(1)}, u32[]{:S(2)}, u32[]{:S(2)}) async-start(bf16[8,2,1024]{2,1,0:T(2,128)(2,1)} %reshape.435), calls=%async_computation.2 | async-start | bytes 65536 | tf_op jit(solution)/shard_map/all_to_all | solution.py:66
  33.5 0.7 %copy-start.3 = (f32[64]{0:T(128)S(1)}, f32[64]{0:T(128)}, u32[]{:S(2)}) copy-start(f32[64]{0:T(128)} %param.11) | copy-start | bytes 772
  33.5 0.7 %copy-start.4 = (f32[64]{0:T(128)S(1)}, f32[64]{0:T(128)}, u32[]{:S(2)}) copy-start(f32[64]{0:T(128)} %param.10) | copy-start | bytes 772
where the time goes:
time: 52 us; the launch traced here: 51.4 us
  starting transfers between devices  16.8 us (32%)
  waiting for transfers between devices  10.6 us (20%)
  blocking collectives  9.06 us (17%)
  other arithmetic  7.48 us (14%)
  local copies, waits for them, and re-layouts  6.8 us (13%)
  matrix products  0.54 us (1%)
    all_to_all x1, blocking collectives, body(): lax.all_to_all(for_sending(result), ('seqa', 'seqb'), split_axis=0, conca...  9.06 us
    all_to_all x1, starting transfers between devices, body(): lax.all_to_all(queries, ('seqa', 'seqb'), split_axis=1, concat_axis=0, ti...  7.41 us
    all_to_all x1, waiting for transfers between devices, body(): lax.all_to_all(keys, ('seqa', 'seqb'), split_axis=1, concat_axis=0, tiled...  6.22 us
    all_to_all x1, starting transfers between devices, body(): lax.all_to_all(keys, ('seqa', 'seqb'), split_axis=1, concat_axis=0, tiled...  6 us
    unnamed x25, local copies, waits for them, and re-layouts  4.6 us
    gather x2, other arithmetic, attend_head(): positions = places - doc_bounds[doc]  4.39 us
    all_to_all x1, waiting for transfers between devices, body(): lax.all_to_all(values, ('seqa', 'seqb'), split_axis=1, concat_axis=0, til...  4.37 us
    all_to_all x1, starting transfers between devices, body(): lax.all_to_all(values, ('seqa', 'seqb'), split_axis=1, concat_axis=0, til...  3.34 us
  transfers between devices with their start and end apart: 3, of which 2 were waited for; matrix products, arithmetic and copies ran while one was open for 19% of the time, Pallas kernels for 0%

commit v1 on v0

--- a/solution.py
+++ b/solution.py
@@ -60,10 +60,13 @@
 
 
 def body(queries, keys, values, doc_bounds, q_gain, k_gain):
+    results_raise = lambda vec, mesh_dim: jnp.concatenate(
+        lax.all_to_all(jnp.stack(jnp.split(vec, lax.axis_size(mesh_dim), 1)), mesh_dim, 0, 0), 0
+    )
     query_full, key_full, value_full = (
         lax.all_to_all(queries, ("seqa", "seqb"), split_axis=1, concat_axis=0, tiled=True),
         lax.all_to_all(keys, ("seqa", "seqb"), split_axis=1, concat_axis=0, tiled=True),
-        lax.all_to_all(values, ("seqa", "seqb"), split_axis=1, concat_axis=0, tiled=True),
+        results_raise(values, ("seqa", "seqb")),
     )
     attend_all = jax.vmap(attend_head, in_axes=(1, 1, 1, None, None, None), out_axes=1)
     result = attend_all(query_full, key_full, value_full, doc_bounds, q_gain, k_gain)

time: 52 us -> 52.2 us (level)
    unnamed x25 -> x31, local copies, waits for them, and re-layouts: 4.6 us -> 4.65 us
  transfers between devices with their start and end apart: 3 -> 3, of which waited for: 2 -> 2; matrix products, arithmetic and copies ran while one was open for 19% -> 20% of each run, Pallas kernels for 0% -> 0%
where the time goes in v1:
time: 52.2 us; the launch traced here: 51.6 us
  starting transfers between devices  16.8 us (32%)
  waiting for transfers between devices  10.6 us (20%)
  blocking collectives  9.06 us (17%)
  other arithmetic  7.48 us (14%)
  local copies, waits for them, and re-layouts  6.98 us (13%)
  matrix products  0.54 us (1%)
    all_to_all x1, blocking collectives, body(): lax.all_to_all(for_sending(result), ('seqa', 'seqb'), split_axis=0, conca...  9.06 us
    all_to_all x1, starting transfers between devices, body(): lax.all_to_all(queries, ('seqa', 'seqb'), split_axis=1, concat_axis=0, ti...  7.41 us
    all_to_all x1, waiting for transfers between devices, body(): lax.all_to_all(keys, ('seqa', 'seqb'), split_axis=1, concat_axis=0, tiled...  6.22 us
    all_to_all x1, starting transfers between devices, body(): lax.all_to_all(keys, ('seqa', 'seqb'), split_axis=1, concat_axis=0, tiled...  6 us
    unnamed x31, local copies, waits for them, and re-layouts  4.65 us
    gather x2, other arithmetic, attend_head(): positions = places - doc_bounds[doc]  4.39 us
    all_to_all x1, waiting for transfers between devices, body(): lax.all_to_all(jnp.stack(jnp.split(vec, lax.axis_size(mesh_dim), 1)), mes...  4.37 us
    all_to_all x1, starting transfers between devices, body(): lax.all_to_all(jnp.stack(jnp.split(vec, lax.axis_size(mesh_dim), 1)), mes...  3.34 us
  transfers between devices with their start and end apart: 3, of which 2 were waited for; matrix products, arithmetic and copies ran while one was open for 20% of the time, Pallas kernels for 0%

profile of v1, /device:TPU:0, one launch (start us, length us, event | category | flops | bytes accessed | tf_op | source)
XLA Modules:
  0.0 51.6 jit_solution(15404405116002688660)
XLA Ops:
  0.0 0.8 %copy.97 = bf16[32,8,64]{2,0,1:T(8,128)(2,1)S(1)} copy(bf16[32,8,64]{2,1,0:T(8,128)(2,1)} %param.6) | data formatting | bytes 65536 | tf_op args[0]
  0.9 0.7 %reshape.436 = bf16[8,2,1024]{2,1,0:T(2,128)(2,1)} reshape(bf16[8,32,64]{2,1,0:T(8,128)(2,1)S(1)} %bitcast.95) | data formatting | bytes 65536
  1.6 7.4 %all-to-all-start = ((bf16[8,2,1024]{2,1,0:T(2,128)(2,1)}), bf16[8,2,1024]{2,1,0:T(2,128)(2,1)S(1)}, u32[]{:S(2)}, u32[]{:S(2)}) async-start(bf16[8,2,1024]{2,1,0:T(2,128)(2,1)} %reshape.436), calls=%async_computation | async-start | bytes 65536 | tf_op jit(solution)/shard_map/all_to_all | solution.py:67
  9.0 0.7 %fusion.36 = (s32[1]{0:T(128)}, s32[1]{0:T(128)}, s32[1]{0:T(128)}, s32[1]{0:T(128)}, s32[1]{0:T(128)}, /*index=5*/s32[1]{0:T(128)}, s32[1]{0:T(128)}, s32[1]{0:T(128)}, s32[1]{0:T(128)}) fusion(s32[9]{0:T(128)S(1)} %copy-done.2), kind=kLoop, calls=%fused_computation.78 | loop fusion | bytes 72 | tf_op jit(solution)/shard_map/vmap()/gather | solution.py:37
  9.9 0.7 %reshape.438 = bf16[8,2,1024]{2,1,0:T(2,128)(2,1)} reshape(bf16[8,32,64]{2,1,0:T(8,128)(2,1)S(1)} %bitcast.96) | data formatting | bytes 65536
  10.6 0.1 copy-done
  11.0 0.7 %reshape.434 = bf16[8,2,1024]{2,1,0:T(2,128)(2,1)} reshape(bf16[8,1,32,64]{3,2,1,0:T(8,128)(2,1)S(1)} %bitcast.97) | data formatting | bytes 65536
  11.7 4.4 %compare_select_fusion.1 = s32[256,1]{0,1:T(1,128)S(1)} fusion(s32[]{:T(128)} %bitcast.7, s32[]{:T(128)} %bitcast.8, s32[]{:T(128)} %bitcast.9, s32[]{:T(128)} %bitcast.10, s32[]{:T(128)} %bitcast.11, s32[]{:T(128)} %bitcast.13, s32[]{:T(128)} %bitcast.12, s32[256,1]{0,1:T(1,128)S(1)} %bitcast.100), kind=kLoop, calls=%fused_computation.66 | loop fusion | flops 3840 | bytes 2076 | tf_op jit(solution)/shard_map/vmap()/gather | solution.py:37
  16.1 1.2 %fusion.32 = f32[256]{0:T(256)S(1)} fusion(pred[256]{0:T(512)(128)(4,1)S(1)} %get-tuple-element.22, pred[256]{0:T(512)(128)(4,1)S(1)} %get-tuple-element.21, s32[256]{0:T(256)S(1)} %bitcast.101, s32[]{:T(128)} %bitcast.5, s32[]{:T(128)} %bitcast.6), kind=kLoop, calls=%fused_computation.73 | loop fusion | flops 1024 | bytes 2568 | tf_op jit(solution)/shard_map/vmap()/convert_element_type | solution.py:20
  17.3 6.0 %all-to-all-start.1 = ((bf16[8,2,1024]{2,1,0:T(2,128)(2,1)}), bf16[8,2,1024]{2,1,0:T(2,128)(2,1)S(1)}, u32[]{:S(2)}, u32[]{:S(2)}) async-start(bf16[8,2,1024]{2,1,0:T(2,128)(2,1)} %reshape.438), calls=%async_computation.1 | async-start | bytes 65536 | tf_op jit(solution)/shard_map/all_to_all | solution.py:68
  23.8 6.2 %all-to-all-done.1 = bf16[8,2,1024]{2,1,0:T(2,128)(2,1)S(1)} async-done(((bf16[8,2,1024]{2,1,0:T(2,128)(2,1)}), bf16[8,2,1024]{2,1,0:T(2,128)(2,1)S(1)}, u32[]{:S(2)}, u32[]{:S(2)}) %all-to-all-start.1) | async-done | bytes 32800 | tf_op jit(solution)/shard_map/all_to_all | solution.py:68
  30.0 3.3 %all-to-all-start.2 = ((bf16[8,2,1024]{2,1,0:T(2,128)(2,1)}), bf16[8,2,1024]{2,1,0:T(2,128)(2,1)S(1)}, u32[]{:S(2)}, u32[]{:S(2)}) async-start(bf16[8,2,1024]{2,1,0:T(2,128)(2,1)} %reshape.434), calls=%async_computation.2 | async-start | bytes 65536 | tf_op jit(solution)/shard_map/all_to_all | solution.py:64
  33.8 0.6 %copy-done.3 = f32[64]{0:T(128)S(1)} copy-done((f32[64]{0:T(128)S(1)}, f32[64]{0:T(128)}, u32[]{:S(2)}) %copy-start.3) | copy-done | bytes 280
  34.4 0.1 fusion.20
  34.6 0.6 %fusion.29 = (bf16[256,32]{1,0:T(8,128)(2,1)S(1)}, bf16[256,32]{1,0:T(8,128)(2,1)S(1)}, bf16[256,32]{1,0:T(8,128)(2,1)S(1)}, bf16[256,32]{1,0:T(8,128)(2,1)S(1)}) fusion(f32[1,256,64]{2,1,0:T(8,128)S(1)} %get-tuple-element.59, f32[32]{0:T(128)S(1)} %multiply_exponential_fusion, f32[256]{0:T(256)S(1)} %fusion.32, f32[1,256,64]{2,1,0:T(8,128)S(1)} %get-tuple-element.60), kind=kLoop, calls=%fused_computation.40 | loop fusion | flops 139264 | bytes 197760 | tf_op jit(solution)/shard_map/vmap()/concatenate | solution.py:25
  35.2 0.3 fusion.37
  35.5 0.1 fusion.11
  35.6 4.4 %all-to-all-done.2 = bf16[8,2,1024]{2,1,0:T(2,128)(2,1)S(1)} async-done(((bf16[8,2,1024]{2,1,0:T(2,128)(2,1)}), bf16[8,2,1024]{2,1,0:T(2,128)(2,1)S(1)}, u32[]{:S(2)}, u32[]{:S(2)}) %all-to-all-start.2) | async-done | bytes 32800 | tf_op jit(solution)/shard_map/all_to_all | solution.py:64
  40.1 0.2 fusion.1
  40.4 0.5 broadcast.313
  40.9 0.7 %reduce.16 = bf16[256,64]{0,1:T(8,128)(2,1)S(1)} reduce(bf16[256,1,64]{0,2,1:T(8,128)(2,1)S(1)} %fusion.1, bf16[]{:T(256)} %broadcast.313), dimensions={1}, to_apply=%copy.57.reduce_sub_computation | reduce | bytes 65538 | tf_op jit(solution)/shard_map/vmap()/transpose;vmap()/reshape;vmap()/transpose | solution.py:72
  41.6 0.1 reshape.440
  41.8 9.1 %all_to_all.41 = bf16[8,2,1024]{2,1,0:T(2,128)(2,1)S(1)} all-to-all(bf16[8,2,1024]{2,1,0:T(2,128)(2,1)S(1)} %reshape.440), channel_id=1, replica_groups=mesh['seqa'=4,'seqb'=2,'dp'=4] {'seqa','seqb'}, dimensions={0} | all-to-all | bytes 65536 | tf_op jit(solution)/shard_map/all_to_all | solution.py:75
  51.0 0.7 %copy.58 = bf16[32,8,64]{2,1,0:T(8,128)(2,1)} copy(bf16[32,8,64]{2,0,1:T(8,128)(2,1)S(1)} %bitcast.94) | data formatting | bytes 65536 | tf_op jit(solution)/shard_map/all_to_all | solution.py:75
  (39 shorter events, 1.7 us)
Async XLA Ops:
  0.9 8.1 %copy-start.2 = (s32[9]{0:T(128)S(1)}, s32[9]{0:T(128)}, u32[]{:S(2)}) copy-start(s32[9]{0:T(128)} %param.9) | copy-start | bytes 112
  1.6 8.3 %copy-start.1 = (bf16[32,8,64]{2,1,0:T(8,128)(2,1)S(1)}, bf16[32,8,64]{2,1,0:T(8,128)(2,1)}, u32[]{:S(2)}) copy-start(bf16[32,8,64]{2,1,0:T(8,128)(2,1)} %param.7) | copy-start | bytes 98308
  1.6 15.7 %all-to-all-start = ((bf16[8,2,1024]{2,1,0:T(2,128)(2,1)}), bf16[8,2,1024]{2,1,0:T(2,128)(2,1)S(1)}, u32[]{:S(2)}, u32[]{:S(2)}) async-start(bf16[8,2,1024]{2,1,0:T(2,128)(2,1)} %reshape.436), calls=%async_computation | async-start | bytes 65536 | tf_op jit(solution)/shard_map/all_to_all | solution.py:67
  9.9 0.8 %copy-start = (bf16[32,8,64]{2,1,0:T(8,128)(2,1)S(1)}, bf16[32,8,64]{2,1,0:T(8,128)(2,1)}, u32[]{:S(2)}) copy-start(bf16[32,8,64]{2,1,0:T(8,128)(2,1)} %param.8) | copy-start | bytes 98308
  17.3 12.7 %all-to-all-start.1 = ((bf16[8,2,1024]{2,1,0:T(2,128)(2,1)}), bf16[8,2,1024]{2,1,0:T(2,128)(2,1)S(1)}, u32[]{:S(2)}, u32[]{:S(2)}) async-start(bf16[8,2,1024]{2,1,0:T(2,128)(2,1)} %reshape.438), calls=%async_computation.1 | async-start | bytes 65536 | tf_op jit(solution)/shard_map/all_to_all | solution.py:68
  30.0 10.0 %all-to-all-start.2 = ((bf16[8,2,1024]{2,1,0:T(2,128)(2,1)}), bf16[8,2,1024]{2,1,0:T(2,128)(2,1)S(1)}, u32[]{:S(2)}, u32[]{:S(2)}) async-start(bf16[8,2,1024]{2,1,0:T(2,128)(2,1)} %reshape.434), calls=%async_computation.2 | async-start | bytes 65536 | tf_op jit(solution)/shard_map/all_to_all | solution.py:64
  33.8 0.7 %copy-start.3 = (f32[64]{0:T(128)S(1)}, f32[64]{0:T(128)}, u32[]{:S(2)}) copy-start(f32[64]{0:T(128)} %param.11) | copy-start | bytes 772
  33.8 0.7 %copy-start.4 = (f32[64]{0:T(128)S(1)}, f32[64]{0:T(128)}, u32[]{:S(2)}) copy-start(f32[64]{0:T(128)} %param.10) | copy-start | bytes 772
